TPU v7x, 32 devices: a whole 2x2x4 slice. The times are simulated.
32 devices in a mesh: dp: 4 (over z), neg: 8 (over y, x, core).
Axes of the slice: x: 2, y: 2, z: 4, core: 2. Of those that a mesh axis runs over, the one named last changes fastest.
Arguments:
- query_emb: bfloat16 [128, 32, 128], P(('dp', 'neg')), may hold values from -6 to 6
- positive: int32 [128], P(('dp', 'neg')), may hold values from 0 to 31
- passage_emb: bfloat16 [32, 512, 128], P(('dp', 'neg')), may hold values from -6 to 6
- lengths: int32 [32], P(('dp', 'neg')), may hold values from 256 to 512
- residual: bfloat16 [16384, 1024], P(('dp', 'neg')), may hold values from -6 to 6
- context: bfloat16 [16384, 1024], P(('dp', 'neg')), may hold values from -6 to 6
- out_proj: bfloat16 [1024, 1024], replicated, may hold values from -0.1875 to 0.1875
- norm_gain: float32 [1024], replicated, may hold values from 0.5 to 1.5
- colbert_proj: bfloat16 [1024, 128], replicated, may hold values from -0.1875 to 0.1875
Outputs:
- loss: float32 [], replicated
- query_grad: float32 [128, 32, 128], P(('dp', 'neg'))
- residual_grad: bfloat16 [16384, 1024], P(('dp', 'neg'))
- context_grad: bfloat16 [16384, 1024], P(('dp', 'neg'))
- out_proj_grad: float32 [1024, 1024], replicated
- colbert_grad: float32 [1024, 128], replicated
- gain_grad: float32 [1024], replicated
Inputs may be any that keep to these rules, and one draw needn't show every extreme that they name: A passage's first lengths[p] token slots are real, the rest padding.
All inputs are finite; a program needn't handle non-finite values.
Results may differ from a plain program's by a relative error of at most 0.0065.
Values may be sent and summed in bfloat16 or wider, within the bound.
A program may use at most 64 MiB of HBM per device.

v0:
```python
import math
import jax
import jax.numpy as jnp
from jax import lax
from jax.sharding import PartitionSpec as P


def combined_all(array, axis, combine):
    everything = jax.tree.map(lambda part: lax.all_gather(part, axis), array)
    initial = jax.tree.map(lambda part: part[0], everything)

    def turn(k, so_far):
        return combine(so_far, jax.tree.map(lambda part: part[k], everything))

    return lax.fori_loop(1, lax.axis_size(axis), turn, initial)


def block_plan(query_count, query_len):
    return math.gcd(query_count, max(1, 2048 // query_len))


def masked_scores(query_block, passage_one, usable):
    scores = jnp.einsum("rd,jd->rj", query_block, passage_one, preferred_element_type=jnp.float32)
    return jnp.where(usable, scores, -1e30)


def tile_forward(query_tokens, query_pos, passage_tokens, passage_len, passage_ids):
    query_count, query_len, emb_width = query_tokens.shape
    per_block = block_plan(query_count, query_len)
    query_blocks = query_tokens.reshape(query_count // per_block, per_block * query_len, emb_width)

    def per_passage(inputs):
        passage_one, length = inputs
        usable = (jnp.arange(passage_one.shape[0]) < length)[None, :]

        def per_query(query_block):
            masked = masked_scores(query_block, passage_one, usable)
            highest = jnp.max(masked, axis=1, keepdims=True)
            return highest[:, 0] + jnp.log(jnp.sum(jnp.exp(masked - highest), axis=1))

        inner_lse = lax.map(per_query, query_blocks).reshape(query_count, query_len)
        shifted = inner_lse - jnp.log(length.astype(jnp.float32))
        return (inner_lse, jnp.sum(shifted, axis=1))

    inner_all, similar = lax.map(per_passage, (passage_tokens, passage_len))
    similar = similar.T
    is_positive = passage_ids[None, :] == query_pos[:, None]
    highest = jnp.max(similar, axis=1)
    exp_total = jnp.sum(jnp.exp(similar - highest[:, None]), axis=1)
    positive_score = jnp.sum(jnp.where(is_positive, similar, 0.0), axis=1)
    return (inner_all, similar, is_positive, (highest, exp_total, positive_score))


def combine_totals(earlier, later):
    highest = jnp.maximum(earlier[0], later[0])
    exp_total = earlier[1] * jnp.exp(earlier[0] - highest) + later[1] * jnp.exp(later[0] - highest)
    return (highest, exp_total, earlier[2] + later[2])


def finish_rows(similar, is_positive, totals, own_block, query_dev):
    log_total = totals[0] + jnp.log(totals[1])
    coefficient = jnp.exp(similar - log_total[:, None]) - is_positive.astype(jnp.float32)
    own_terms = lax.dynamic_slice_in_dim(log_total - totals[2], own_block * query_dev, query_dev)
    return (coefficient, jnp.sum(own_terms))


def tile_backward(query_tokens, passage_tokens, passage_len, inner_all, coefficient):
    query_count, query_len, emb_width = query_tokens.shape
    per_block = block_plan(query_count, query_len)
    block_count = query_count // per_block
    query_blocks = query_tokens.reshape(block_count, per_block * query_len, emb_width)

    def per_passage(running, inputs):
        passage_one, length, inner_lse, column = inputs
        usable = (jnp.arange(passage_one.shape[0]) < length)[None, :]

        def per_query(pieces):
            query_block, inner_block, column_block = pieces
            masked = masked_scores(query_block, passage_one, usable)
            spread = jnp.exp(masked - inner_block.reshape(-1)[:, None]).reshape(
                per_block, query_len, -1
            )
            weight = (
                (spread * column_block[:, None, None])
                .reshape(per_block * query_len, -1)
                .astype(jnp.bfloat16)
            )
            query_part = jnp.dot(weight, passage_one, preferred_element_type=jnp.float32)
            passage_part = jnp.einsum(
                "rj,rd->jd", weight, query_block, preferred_element_type=jnp.float32
            )
            return (query_part, passage_part)

        query_parts, passage_parts = lax.map(
            per_query,
            (
                query_blocks,
                inner_lse.reshape(block_count, per_block, query_len),
                column.reshape(block_count, per_block),
            ),
        )
        return (running + query_parts.reshape(running.shape), jnp.sum(passage_parts, axis=0))

    start = jnp.zeros((query_count * query_len, emb_width), jnp.float32)
    query_sum, passage_sum = lax.scan(
        per_passage, start, (passage_tokens, passage_len, inner_all, coefficient.T)
    )
    return (query_sum.reshape(query_count, query_len, emb_width), passage_sum)


def window_rows(resid_rows, context_rows, grad_rows, out_proj, norm_gain, colbert_proj):
    hidden = resid_rows.astype(jnp.float32) + jnp.dot(
        context_rows, out_proj, preferred_element_type=jnp.float32
    )
    row_mean = jnp.mean(hidden, axis=1, keepdims=True)
    centred = hidden - row_mean
    variance = jnp.mean(centred * centred, axis=1, keepdims=True)
    inv_std = 1.0 / jnp.sqrt(variance + 1e-05)
    normed = centred * inv_std
    scaled = (normed * norm_gain).astype(jnp.bfloat16)
    colbert_part = jnp.dot(scaled.T, grad_rows, preferred_element_type=jnp.float32)
    scaled_grad = jnp.dot(grad_rows, colbert_proj.T, preferred_element_type=jnp.float32)
    gain_part = jnp.sum(scaled_grad * normed, axis=0)
    gained = scaled_grad * norm_gain
    hidden_grad = (
        inv_std
        * (
            gained
            - jnp.mean(gained, axis=1, keepdims=True)
            - normed * jnp.mean(gained * normed, axis=1, keepdims=True)
        )
    ).astype(jnp.bfloat16)
    context_grad = jnp.dot(hidden_grad, out_proj.T, preferred_element_type=jnp.float32).astype(
        jnp.bfloat16
    )
    proj_part = jnp.dot(context_rows.T, hidden_grad, preferred_element_type=jnp.float32)
    return (hidden_grad, context_grad, proj_part, colbert_part, gain_part)


def body(
    query_emb, positive, passage_emb, lengths, residual, context, out_proj, norm_gain, colbert_proj
):
    query_dev = query_emb.shape[0]
    passage_dev = passage_emb.shape[0]
    neg_size = lax.axis_size("neg")
    neg_place = lax.axis_index("neg")
    query_tokens, query_pos = (
        lax.all_gather(query_emb, "neg", axis=0, tiled=True),
        lax.all_gather(positive, "neg", axis=0, tiled=True),
    )
    passage_tokens, passage_len = (
        lax.all_gather(passage_emb, "dp", axis=0, tiled=True),
        lax.all_gather(lengths, "dp", axis=0, tiled=True),
    )
    position = jnp.arange(passage_tokens.shape[0], dtype=jnp.int32)
    passage_ids = (
        position // passage_dev * neg_size + neg_place
    ) * passage_dev + position % passage_dev
    inner_all, similar, is_positive, stats = tile_forward(
        query_tokens, query_pos, passage_tokens, passage_len, passage_ids
    )
    totals = combined_all(stats, "neg", combine_totals)
    coefficient, loss_part = finish_rows(similar, is_positive, totals, neg_place, query_dev)
    query_sum, passage_sum = tile_backward(
        query_tokens, passage_tokens, passage_len, inner_all, coefficient
    )
    query_grad = lax.psum_scatter(query_sum, "neg", scatter_dimension=0, tiled=True)
    emb_sum = lax.psum_scatter(passage_sum, "dp", scatter_dimension=0, tiled=True)
    emb_grad = emb_sum.astype(jnp.bfloat16).reshape(
        passage_dev * emb_sum.shape[1], emb_sum.shape[2]
    )
    residual_grad, context_grad, proj_part, colbert_part, gain_part = window_rows(
        residual, context, emb_grad, out_proj, norm_gain, colbert_proj
    )
    out_proj_grad, colbert_grad, gain_grad, loss_total = lax.psum(
        (proj_part, colbert_part, gain_part, loss_part), ("dp", "neg")
    )
    loss = loss_total / (query_dev * lax.axis_size("dp") * neg_size)
    return (loss, query_grad, residual_grad, context_grad, out_proj_grad, colbert_grad, gain_grad)


def solution(mesh):
    in_specs = (
        P(("dp", "neg"), None, None),
        P(("dp", "neg")),
        P(("dp", "neg"), None, None),
        P(("dp", "neg")),
        P(("dp", "neg"), None),
        P(("dp", "neg"), None),
        P(),
        P(),
        P(),
    )
    out_specs = (
        P(),
        P(("dp", "neg"), None, None),
        P(("dp", "neg"), None),
        P(("dp", "neg"), None),
        P(),
        P(),
        P(),
    )
    return jax.shard_map(body, mesh=mesh, in_specs=in_specs, out_specs=out_specs, check_vma=False)
```

profile of v0, /device:TPU:0, one launch (start us, length us, event | category | flops | bytes accessed | tf_op | source)
XLA Modules:
  0.0 304.9 jit_solution(8071022490365719969)
XLA Ops:
  10.9 9.9 %all-reduce = s32[4]{0:T(128)S(1)} all-reduce(s32[4]{0:T(128)S(1)} %dynamic-update-slice), channel_id=1, replica_groups=mesh['dp'=4,'neg'=8] {'dp'}, use_global_device_ids=true, to_apply=%add | all-reduce | flops 4 | bytes 32
  20.8 16.9 %all_gather.31 = bf16[4,512,128]{2,1,0:T(8,128)(2,1)} all-gather(bf16[1,512,128]{2,1,0:T(8,128)(2,1)} %param.17), channel_id=1, replica_groups=mesh['dp'=4,'neg'=8] {'dp'}, dimensions={0}, use_global_device_ids=true | all-gather | bytes 655360 | tf_op jit(solution)/shard_map/all_gather | solution.py:152
  37.7 9.5 %all_gather.32 = bf16[32,32,128]{2,1,0:T(8,128)(2,1)S(1)} all-gather(bf16[4,32,128]{2,1,0:T(8,128)(2,1)} %param.15), channel_id=1, replica_groups=mesh['dp'=4,'neg'=8] {'neg'}, dimensions={0}, use_global_device_ids=true | all-gather | bytes 294912 | tf_op jit(solution)/shard_map/all_gather | solution.py:148
  47.2 16.2 %while.53 = (s32[]{:T(128)}, f32[4,32,32]{2,1,0:T(8,128)S(1)}, f32[4,32]{1,0:T(4,128)S(1)}, s32[4]{0:T(128)S(1)}, bf16[4,512,128]{2,1,0:T(8,128)(2,1)}, /*index=...) while((s32[]{:T(128)}, f32[4,32,32]{2,1,0:T(8,128)S(1)}, f32[4,32]{1,0:T(4,128)S(1)}, ...), condition=%wide.region_4.5_spmd, body=%wide.region_0.4_spmd.sunk | while | flops 136840672 | bytes 4672013 | solution.py:45
  64.9 7.1 %all-reduce.3 = s32[32]{0:T(128)S(1)} all-reduce(s32[32]{0:T(128)S(1)} %dynamic-update-slice.3), channel_id=1, replica_groups=mesh['dp'=4,'neg'=8] {'neg'}, use_global_device_ids=true, to_apply=%add.3 | all-reduce | flops 32 | bytes 256
  73.4 11.8 %all-reduce.7 = (f32[256]{0:T(256)S(1)}, f32[256]{0:T(256)S(1)}, f32[256]{0:T(256)S(1)}) all-reduce(f32[256]{0:T(256)S(1)} %dynamic-update-slice.1, f32[256]{0:T(256)S(1)} %dynamic-update-slice.2, f32[256]{0:T(256)S(1)} %dynamic-update-slice.4), channel_id=2, replica_groups=mesh['dp'=4,'neg'=8] {'neg'}, use_global_device_ids=true, to_apply=%add.1 | all-reduce | flops 768 | bytes 6144
  85.8 25.8 %while.55 = (s32[]{:T(128)}, f32[1024,128]{1,0:T(8,128)}, f32[4,512,128]{2,1,0:T(8,128)}, s32[4]{0:T(128)S(1)}, bf16[4,512,128]{2,1,0:T(8,128)(2,1)}, /*index=5*...) while((s32[]{:T(128)}, f32[1024,128]{1,0:T(8,128)}, ...), condition=%wide.region_13.14_spmd.clone, body=%wide.region_12.13_spmd.clone.sunk | while | flops 405012992 | bytes 5282823 | solution.py:105
  87.3 1.5 multiply_convert_fusion.5
  90.0 2.2 convolution_add_fusion.2
  93.6 1.5 multiply_convert_fusion.5
  96.2 2.4 convolution_add_fusion.2
  100.1 1.5 multiply_convert_fusion.5
  102.7 2.4 convolution_add_fusion.2
  106.6 1.5 multiply_convert_fusion.5
  109.2 2.4 convolution_add_fusion.2
  111.7 2.9 fusion.36
  116.2 21.0 %reduce-scatter.5.cloned.1.call-done = f32[1,512,128]{2,1,0:T(8,128)} async-done(((f32[4,512,128]{2,1,0:T(8,128)}), f32[1,512,128]{2,1,0:T(8,128)}) %reduce-scatter.5.cloned.1.call-update) | async-done | bytes 262160 | tf_op jit(solution)/shard_map/reduce_scatter | solution.py:168
  137.3 2.7 multiply_reduce_fusion
  141.2 3.3 %convolution_bitcast_fusion.1 = f32[1024,1024]{0,1:T(8,128)} fusion(bf16[512,1024]{1,0:T(8,128)(2,1)S(1)} %multiply_convert_fusion.2, bf16[512,1024]{1,0:T(8,128)(2,1)S(1)} %copy-done.5), kind=kOutput, calls=%fused_computation.37 | convolution fusion | flops 1073741824 | bytes 6291456 | tf_op jit(solution)/shard_map/dot_general | solution.py:136
  144.5 1.6 fusion.22
  147.4 39.7 %all-reduce.5 = (f32[]{:T(128)}, f32[1024]{0:T(1024)}) all-reduce(f32[]{:T(128)} %dynamic-slice_reduce_fusion, f32[1024]{0:T(1024)S(1)} %get-tuple-element.355), channel_id=1, replica_groups=mesh['dp'=4,'neg'=8] {'dp','neg'}, use_global_device_ids=true, to_apply=%region_11.12 | all-reduce | flops 1025 | bytes 8200 | tf_op jit(solution)/shard_map/psum | solution.py:175
  187.7 2.3 convolution_convert_fusion
  190.0 100.1 %all-reduce.10.cloned.1.call-done = (f32[1024,1024]{0,1:T(8,128)}, f32[1024,128]{1,0:T(8,128)}) async-done(((f32[1024,1024]{0,1:T(8,128)}, f32[1024,128]{1,0:T(8,128)}), (f32[1024,1024]{0,1:T(8,128)}, f32[1024,128]{1,0:T(8,128)})) %all-reduce.10.cloned.1.call-update) | async-done | bytes 4718608 | tf_op jit(solution)/shard_map/psum | solution.py:175
  290.1 5.4 %copy.18 = f32[1024,1024]{1,0:T(8,128)} copy(f32[1024,1024]{0,1:T(8,128)} %get-tuple-element.404) | data formatting | bytes 8388608
  (143 shorter events, 33.2 us)
Async XLA Ops:
  8.0 103.7 %copy-start = (bf16[1024,1024]{1,0:T(8,128)(2,1)S(1)}, bf16[1024,1024]{1,0:T(8,128)(2,1)}, u32[]{:S(2)}) copy-start(bf16[1024,1024]{1,0:T(8,128)(2,1)} %param.21) | copy-start | bytes 6291460
  8.0 129.2 %reduce-scatter.5.cloned.1.call-start = ((), (), s32[]{:S(2)}) async-start(), calls=%async_computation.3 | async-start | bytes 1310720 | tf_op jit(solution)/shard_map/reduce_scatter | solution.py:168
  47.2 16.2 %copy-start.10 = (u32[32]{0:T(128)S(1)}, u32[32]{0:T(128)}, u32[]{:S(2)}) copy-start(u32[32]{0:T(128)} %constant.164) | copy-start | bytes 388
  47.2 17.5 %copy-start.9 = (s32[4]{0:T(128)S(1)}, s32[4]{0:T(128)}, u32[]{:S(2)}) copy-start(s32[4]{0:T(128)} %param.16) | copy-start | bytes 52
  111.6 178.5 %all-reduce.10.cloned.1.call-start = ((), (), s32[]{:S(2)}) async-start(), calls=%async_computation.4 | async-start | bytes 9437184 | tf_op jit(solution)/shard_map/psum | solution.py:175
  114.6 1.3 copy-start.1
  114.6 22.7 %copy-start.7 = (bf16[1024,128]{1,0:T(8,128)(2,1)S(1)}, bf16[1024,128]{1,0:T(8,128)(2,1)}, u32[]{:S(2)}) copy-start(bf16[1024,128]{1,0:T(8,128)(2,1)} %param.23) | copy-start | bytes 786436
  114.6 22.7 %copy-start.8 = (f32[1024]{0:T(1024)S(1)}, f32[1024]{0:T(1024)}, u32[]{:S(2)}) copy-start(f32[1024]{0:T(1024)} %param.22) | copy-start | bytes 12292
  137.3 2.7 copy-start.2
  140.0 1.2 copy-start.5
  141.2 46.5 %copy-start.3 = (bf16[512,1024]{1,0:T(8,128)(2,1)}, bf16[512,1024]{1,0:T(8,128)(2,1)S(1)}, u32[]{:S(2)}) copy-start(bf16[512,1024]{1,0:T(8,128)(2,1)S(1)} %multiply_convert_fusion.2) | copy-start | bytes 3145732
  141.2 3.3 %copy-start.4 = (f32[1,512,128]{2,1,0:T(8,128)S(1)}, f32[1,512,128]{2,1,0:T(8,128)}, u32[]{:S(2)}) copy-start(f32[1,512,128]{2,1,0:T(8,128)} %reduce-scatter.5.cloned.1.call-done) | copy-start | bytes 786436
  146.1 149.4 %reduce-scatter.3.cloned.1.call-start = ((), (), s32[]{:S(2)}) async-start(), calls=%async_computation.2 | async-start | bytes 589824 | tf_op jit(solution)/shard_map/reduce_scatter | solution.py:167
  290.1 5.4 %copy-start.6 = (f32[1024,128]{1,0:T(8,128)S(1)}, f32[1024,128]{1,0:T(8,128)}, u32[]{:S(2)}) copy-start(f32[1024,128]{1,0:T(8,128)} %get-tuple-element.658) | copy-start | bytes 1572868
Sparse Core Ops, SparseCore 0:
  111.7 25.4 reduce-scatter.4
  146.3 143.7 all-reduce.9
Sparse Core Ops, SparseCore 1:
  150.3 32.6 reduce-scatter.2
where the time goes:
time: 306 us; the launch traced here: 305 us
  waiting for transfers between devices  122 us (40%)
  blocking collectives  94.9 us (31%)
  matrix products  38 us (12%)
  between operations  19.5 us (6%)
  local copies, waits for them, and re-layouts  18.2 us (6%)
  other arithmetic  9.43 us (3%)
  loops' own time  3.07 us (1%)
    psum x1, waiting for transfers between devices, body(): lax.psum((proj_part, colbert_part, gain_part, loss_part), ('dp', 'neg'))  100 us
    psum x1, blocking collectives, body(): lax.psum((proj_part, colbert_part, gain_part, loss_part), ('dp', 'neg'))  39.7 us
    unnamed x3, blocking collectives  28.8 us
    reduce_scatter x1, waiting for transfers between devices, body(): lax.psum_scatter(passage_sum, 'dp', scatter_dimension=0, tiled=True)  21 us
    all_gather x1, blocking collectives, body(): lax.all_gather(passage_emb, 'dp', axis=0, tiled=True)  16.9 us
    unnamed x36, local copies, waits for them, and re-layouts  11.6 us
    dot_general x8, matrix products, masked_scores(): jnp.einsum('rd,jd->rj', query_block, passage_one, preferred_element_type=...  11.4 us
    all_gather x1, blocking collectives, body(): lax.all_gather(query_emb, 'neg', axis=0, tiled=True)  9.51 us
  transfers between devices with their start and end apart: 3, of which 2 were waited for; matrix products, arithmetic and copies ran while one was open for 4% of the time, Pallas kernels for 0%

commit v1 on v0

--- a/solution.py
+++ b/solution.py
@@ -173,7 +173,7 @@
         residual, context, emb_grad, out_proj, norm_gain, colbert_proj
     )
     out_proj_grad, colbert_grad, gain_grad, loss_total = lax.psum(
-        (proj_part, colbert_part, gain_part, loss_part), ("dp", "neg")
+        lax.psum((proj_part, colbert_part, gain_part, loss_part), "dp"), "neg"
     )
     loss = loss_total / (query_dev * lax.axis_size("dp") * neg_size)
     return (loss, query_grad, residual_grad, context_grad, out_proj_grad, colbert_grad, gain_grad)

time: 306 us -> 453 us (1.48)
  waiting for transfers between devices: 122 us -> 286 us
  blocking collectives: 94.9 us -> 79.5 us
    psum x1 -> x2, waiting for transfers between devices: 100 us -> 232 us  [the longest x1 171 us: body(): lax.psum((proj_part, colbert_part, gain_part, loss_part), 'dp')]
    reduce_scatter x1, waiting for transfers between devices: 0.01 us -> 32.3 us  [body(): lax.psum_scatter(query_sum, 'neg', scatter_dimension=0, tiled=True)]
    psum x1 -> x2, blocking collectives: 39.7 us -> 24.3 us  [the longest x1 14.2 us: body(): lax.psum(lax.psum((proj_part, colbert_part, gain_part, loss_part), 'dp'),...]
  transfers between devices with their start and end apart: 3 -> 4, of which waited for: 2 -> 4; matrix products, arithmetic and copies ran while one was open for 4% -> 3% of each run, Pallas kernels for 0% -> 0%
where the time goes in v1:
time: 453 us; the launch traced here: 452 us
  waiting for transfers between devices  286 us (63%)
  blocking collectives  79.5 us (18%)
  matrix products  38 us (8%)
  local copies, waits for them, and re-layouts  18.2 us (4%)
  between operations  17.8 us (4%)
  other arithmetic  9.43 us (2%)
    psum x1, waiting for transfers between devices, body(): lax.psum((proj_part, colbert_part, gain_part, loss_part), 'dp')  171 us
    psum x1, waiting for transfers between devices, body(): lax.psum(lax.psum((proj_part, colbert_part, gain_part, loss_part), 'dp'),...  61.1 us
    reduce_scatter x1, waiting for transfers between devices, body(): lax.psum_scatter(query_sum, 'neg', scatter_dimension=0, tiled=True)  32.3 us
    unnamed x3, blocking collectives  28.8 us
    reduce_scatter x1, waiting for transfers between devices, body(): lax.psum_scatter(passage_sum, 'dp', scatter_dimension=0, tiled=True)  21 us
    all_gather x1, blocking collectives, body(): lax.all_gather(passage_emb, 'dp', axis=0, tiled=True)  16.9 us
    psum x1, blocking collectives, body(): lax.psum(lax.psum((proj_part, colbert_part, gain_part, loss_part), 'dp'),...  14.2 us
    unnamed x36, local copies, waits for them, and re-layouts  11.6 us
  transfers between devices with their start and end apart: 4, of which 4 were waited for; matrix products, arithmetic and copies ran while one was open for 3% of the time, Pallas kernels for 0%

profile of v1, /device:TPU:0, one launch (start us, length us, event | category | flops | bytes accessed | tf_op | source)
XLA Modules:
  0.0 451.7 jit_solution(12295078461135185338)
XLA Ops:
  10.0 9.9 %all-reduce = s32[4]{0:T(128)S(1)} all-reduce(s32[4]{0:T(128)S(1)} %dynamic-update-slice), channel_id=1, replica_groups=mesh['dp'=4,'neg'=8] {'dp'}, use_global_device_ids=true, to_apply=%add | all-reduce | flops 4 | bytes 32
  20.0 16.9 %all_gather.31 = bf16[4,512,128]{2,1,0:T(8,128)(2,1)} all-gather(bf16[1,512,128]{2,1,0:T(8,128)(2,1)} %param.17), channel_id=1, replica_groups=mesh['dp'=4,'neg'=8] {'dp'}, dimensions={0}, use_global_device_ids=true | all-gather | bytes 655360 | tf_op jit(solution)/shard_map/all_gather | solution.py:152
  36.8 9.5 %all_gather.32 = bf16[32,32,128]{2,1,0:T(8,128)(2,1)S(1)} all-gather(bf16[4,32,128]{2,1,0:T(8,128)(2,1)} %param.15), channel_id=1, replica_groups=mesh['dp'=4,'neg'=8] {'neg'}, dimensions={0}, use_global_device_ids=true | all-gather | bytes 294912 | tf_op jit(solution)/shard_map/all_gather | solution.py:148
  46.3 16.2 %while.53 = (s32[]{:T(128)}, f32[4,32,32]{2,1,0:T(8,128)S(1)}, f32[4,32]{1,0:T(4,128)S(1)}, s32[4]{0:T(128)S(1)}, bf16[4,512,128]{2,1,0:T(8,128)(2,1)}, /*index=...) while((s32[]{:T(128)}, f32[4,32,32]{2,1,0:T(8,128)S(1)}, f32[4,32]{1,0:T(4,128)S(1)}, ...), condition=%wide.region_4.5_spmd, body=%wide.region_0.4_spmd.sunk | while | flops 136840672 | bytes 4672013 | solution.py:45
  64.1 7.1 %all-reduce.3 = s32[32]{0:T(128)S(1)} all-reduce(s32[32]{0:T(128)S(1)} %dynamic-update-slice.3), channel_id=1, replica_groups=mesh['dp'=4,'neg'=8] {'neg'}, use_global_device_ids=true, to_apply=%add.3 | all-reduce | flops 32 | bytes 256
  72.6 11.8 %all-reduce.6 = (f32[256]{0:T(256)S(1)}, f32[256]{0:T(256)S(1)}, f32[256]{0:T(256)S(1)}) all-reduce(f32[256]{0:T(256)S(1)} %dynamic-update-slice.1, f32[256]{0:T(256)S(1)} %dynamic-update-slice.2, f32[256]{0:T(256)S(1)} %dynamic-update-slice.4), channel_id=2, replica_groups=mesh['dp'=4,'neg'=8] {'neg'}, use_global_device_ids=true, to_apply=%add.1 | all-reduce | flops 768 | bytes 6144
  85.0 25.8 %while.55 = (s32[]{:T(128)}, f32[1024,128]{1,0:T(8,128)}, f32[4,512,128]{2,1,0:T(8,128)}, s32[4]{0:T(128)S(1)}, bf16[4,512,128]{2,1,0:T(8,128)(2,1)}, /*index=5*...) while((s32[]{:T(128)}, f32[1024,128]{1,0:T(8,128)}, ...), condition=%wide.region_14.15_spmd.clone, body=%wide.region_13.14_spmd.clone.sunk | while | flops 405012992 | bytes 5282823 | solution.py:105
  86.5 1.5 multiply_convert_fusion.5
  89.1 2.2 convolution_add_fusion.2
  95.4 2.4 convolution_add_fusion.2
  101.9 2.4 convolution_add_fusion.2
  108.4 2.4 convolution_add_fusion.2
  110.8 2.9 fusion.36
  115.4 21.0 %reduce-scatter.5.cloned.1.call-done = f32[1,512,128]{2,1,0:T(8,128)} async-done(((f32[4,512,128]{2,1,0:T(8,128)}), f32[1,512,128]{2,1,0:T(8,128)}) %reduce-scatter.5.cloned.1.call-update) | async-done | bytes 262160 | tf_op jit(solution)/shard_map/reduce_scatter | solution.py:168
  136.4 2.7 multiply_reduce_fusion
  140.4 3.3 convolution_bitcast_fusion.1
  143.7 1.6 fusion.22
  145.4 170.6 %all-reduce.15.cloned.1.call-done = (f32[1024,1024]{0,1:T(8,128)}, f32[1024,128]{1,0:T(8,128)}) async-done(((f32[1024,1024]{0,1:T(8,128)}, f32[1024,128]{1,0:T(8,128)}), (f32[1024,1024]{0,1:T(8,128)}, f32[1024,128]{1,0:T(8,128)})) %all-reduce.15.cloned.1.call-update) | async-done | bytes 4718608 | tf_op jit(solution)/shard_map/psum | solution.py:176
  317.2 10.2 %all-reduce.8 = (f32[]{:T(128)}, f32[1024]{0:T(1024)S(1)}) all-reduce(f32[]{:T(128)} %dynamic-slice_reduce_fusion, f32[1024]{0:T(1024)S(1)} %get-tuple-element.355), channel_id=1, replica_groups=mesh['dp'=4,'neg'=8] {'dp'}, use_global_device_ids=true, to_apply=%region_11.12 | all-reduce | flops 1025 | bytes 8200 | tf_op jit(solution)/shard_map/psum | solution.py:176
  327.4 14.2 %all-reduce.5 = (f32[]{:T(128)}, f32[1024]{0:T(1024)}) all-reduce(f32[]{:T(128)} %get-tuple-element.409, f32[1024]{0:T(1024)S(1)} %get-tuple-element.410), channel_id=1, replica_groups=mesh['dp'=4,'neg'=8] {'neg'}, use_global_device_ids=true, to_apply=%region_12.13 | all-reduce | flops 1025 | bytes 8200 | tf_op jit(solution)/shard_map/psum | solution.py:175
  342.2 2.3 convolution_convert_fusion
  344.4 61.1 %all-reduce.13.cloned.1.call-done = (f32[1024,1024]{0,1:T(8,128)}, f32[1024,128]{1,0:T(8,128)}) async-done(((f32[1024,1024]{0,1:T(8,128)}, f32[1024,128]{1,0:T(8,128)}), (f32[1024,1024]{0,1:T(8,128)}, f32[1024,128]{1,0:T(8,128)})) %all-reduce.13.cloned.1.call-update) | async-done | bytes 4718608 | tf_op jit(solution)/shard_map/psum | solution.py:175
  405.5 5.4 %copy.18 = f32[1024,1024]{1,0:T(8,128)} copy(f32[1024,1024]{0,1:T(8,128)} %get-tuple-element.407) | data formatting | bytes 8388608
  410.9 32.3 %reduce-scatter.3.cloned.1.call-done = f32[4,32,128]{2,1,0:T(8,128)} async-done(((f32[32,32,128]{2,1,0:T(8,128)}), f32[4,32,128]{2,1,0:T(8,128)}) %reduce-scatter.3.cloned.1.call-update) | async-done | bytes 65552 | tf_op jit(solution)/shard_map/reduce_scatter | solution.py:167
  (147 shorter events, 37.7 us)
Async XLA Ops:
  7.2 103.7 %copy-start = (bf16[1024,1024]{1,0:T(8,128)(2,1)S(1)}, bf16[1024,1024]{1,0:T(8,128)(2,1)}, u32[]{:S(2)}) copy-start(bf16[1024,1024]{1,0:T(8,128)(2,1)} %param.21) | copy-start | bytes 6291460
  7.2 129.3 %reduce-scatter.5.cloned.1.call-start = ((), (), s32[]{:S(2)}) async-start(), calls=%async_computation.3 | async-start | bytes 1310720 | tf_op jit(solution)/shard_map/reduce_scatter | solution.py:168
  46.3 16.2 %copy-start.10 = (u32[32]{0:T(128)S(1)}, u32[32]{0:T(128)}, u32[]{:S(2)}) copy-start(u32[32]{0:T(128)} %constant.164) | copy-start | bytes 388
  46.3 17.5 %copy-start.9 = (s32[4]{0:T(128)S(1)}, s32[4]{0:T(128)}, u32[]{:S(2)}) copy-start(s32[4]{0:T(128)} %param.16) | copy-start | bytes 52
  110.8 205.1 %all-reduce.15.cloned.1.call-start = ((), (), s32[]{:S(2)}) async-start(), calls=%async_computation.5 | async-start | bytes 9437184 | tf_op jit(solution)/shard_map/psum | solution.py:176
  113.7 1.3 copy-start.1
  113.7 22.7 %copy-start.7 = (bf16[1024,128]{1,0:T(8,128)(2,1)S(1)}, bf16[1024,128]{1,0:T(8,128)(2,1)}, u32[]{:S(2)}) copy-start(bf16[1024,128]{1,0:T(8,128)(2,1)} %param.23) | copy-start | bytes 786436
  113.7 22.7 %copy-start.8 = (f32[1024]{0:T(1024)S(1)}, f32[1024]{0:T(1024)}, u32[]{:S(2)}) copy-start(f32[1024]{0:T(1024)} %param.22) | copy-start | bytes 12292
  136.4 2.7 copy-start.2
  139.2 1.2 copy-start.5
  140.4 201.8 %copy-start.3 = (bf16[512,1024]{1,0:T(8,128)(2,1)}, bf16[512,1024]{1,0:T(8,128)(2,1)S(1)}, u32[]{:S(2)}) copy-start(bf16[512,1024]{1,0:T(8,128)(2,1)S(1)} %multiply_convert_fusion.2) | copy-start | bytes 3145732
  140.4 3.3 copy-start.4
  145.3 260.2 %all-reduce.13.cloned.1.call-start = ((), (), s32[]{:S(2)}) async-start(), calls=%async_computation.4 | async-start | bytes 9437184 | tf_op jit(solution)/shard_map/psum | solution.py:175
  315.9 127.3 %reduce-scatter.3.cloned.1.call-start = ((), (), s32[]{:S(2)}) async-start(), calls=%async_computation.2 | async-start | bytes 589824 | tf_op jit(solution)/shard_map/reduce_scatter | solution.py:167
  405.5 37.7 %copy-start.6 = (f32[1024,128]{1,0:T(8,128)S(1)}, f32[1024,128]{1,0:T(8,128)}, u32[]{:S(2)}) copy-start(f32[1024,128]{1,0:T(8,128)} %get-tuple-element.662) | copy-start | bytes 1572868
Sparse Core Ops, SparseCore 0:
  110.9 25.4 reduce-scatter.4
  145.4 170.4 all-reduce.14
  319.3 86.1 all-reduce.12
  409.0 34.1 reduce-scatter.2
